TPU v7x, 32 devices: a whole 2x2x4 slice. The times are simulated.
32 devices in a mesh: dp: 4 (over x, core), mp: 8 (over z, y).
Axes of the slice: x: 2, y: 2, z: 4, core: 2. Of those that a mesh axis runs over, the one named last changes fastest.
Arguments:
- tokens: bfloat16 [256, 8192], P('dp', 'mp'), may hold values from -80 to 80
- frozen_gate_weight: bfloat16 [8192, 28672], P('mp', 'dp'), may hold values from -0.198873782 to 0.198873782
- frozen_up_weight: bfloat16 [8192, 28672], P('mp', 'dp'), may hold values from -0.198873782 to 0.198873782
- frozen_down_weight: bfloat16 [28672, 8192], P('dp', 'mp'), may hold values from -0.28347335 to 0.28347335
- gate_left_factor: bfloat16 [8192, 16], P('mp'), may hold values from -0.0625 to 0.0625
- gate_right_factor: bfloat16 [16, 28672], P(None, 'dp'), may hold values from -0.75 to 0.75
- up_left_factor: bfloat16 [8192, 16], P('mp'), may hold values from -0.0625 to 0.0625
- up_right_factor: bfloat16 [16, 28672], P(None, 'dp'), may hold values from -0.75 to 0.75
- down_left_factor: bfloat16 [28672, 16], P('dp'), may hold values from -0.03125 to 0.03125
- down_right_factor: bfloat16 [16, 8192], P(None, 'mp'), may hold values from -0.75 to 0.75
- gate_column_magnitude: float32 [28672], P('dp'), may hold values from 0.5 to 2
- up_column_magnitude: float32 [28672], P('dp'), may hold values from 0.5 to 2
- down_column_magnitude: float32 [8192], P('mp'), may hold values from 0.5 to 2
- cotangent: bfloat16 [256, 8192], P('dp', 'mp'), may hold values from -80 to 80
Outputs:
- feedforward_output: bfloat16 [256, 8192], P('dp', 'mp')
- token_input_gradient: bfloat16 [256, 8192], P('dp', 'mp')
- gate_magnitude_gradient: float32 [28672], P('dp')
- up_magnitude_gradient: float32 [28672], P('dp')
- down_magnitude_gradient: float32 [8192], P('mp')
- gate_right_factor_gradient: float32 [16, 28672], P(None, 'dp')
- gate_left_factor_gradient: float32 [8192, 16], P('mp')
- up_right_factor_gradient: float32 [16, 28672], P(None, 'dp')
- up_left_factor_gradient: float32 [8192, 16], P('mp')
- down_right_factor_gradient: float32 [16, 8192], P(None, 'mp')
- down_left_factor_gradient: float32 [28672, 16], P('dp')
All inputs are finite; a program needn't handle non-finite values.
Results may differ from a plain program's by a relative error of at most 0.03.
Values may be sent and summed in bfloat16 or wider, within the bound.
No kernel may reach another device: no remote copies, remote signals or barrier semaphores. Data moves between devices by JAX's collectives and lax.ppermute only.
A program may use at most 192 MiB of HBM per device.

v0:
```python
import jax
import jax.numpy as jnp
from jax import lax
from jax.sharding import PartitionSpec as P

epsilon = 1e-06


def matrix_product(left_side, right_side):
    return jnp.dot(left_side, right_side, preferred_element_type=jnp.float32)


def matrix_product_right_transposed(left_side, right_side):
    return lax.dot_general(
        left_side, right_side, (((1,), (1,)), ((), ())), preferred_element_type=jnp.float32
    )


def matrix_product_left_transposed(left_side, right_side):
    return lax.dot_general(
        left_side, right_side, (((0,), (0,)), ((), ())), preferred_element_type=jnp.float32
    )


def combine_adapter_columns(weight_matrix, left_factor, right_factor):
    combined_weight = weight_matrix.astype(jnp.float32) + matrix_product(left_factor, right_factor)
    return (
        combined_weight.astype(jnp.bfloat16),
        jnp.sum(combined_weight * combined_weight, axis=0),
    )


def activate(pre_pair, scale_gate, scale_up):
    width = scale_gate.shape[0]
    pre_gate = pre_pair[:, :width]
    pre_up = pre_pair[:, width:]
    gate_act = pre_gate * scale_gate
    up_act = pre_up * scale_up
    sigmoid_gate = jax.nn.sigmoid(gate_act)
    silu_gate = gate_act * sigmoid_gate
    hidden_state = (silu_gate * up_act).astype(jnp.bfloat16)
    return (hidden_state, (pre_gate, pre_up, gate_act, up_act, sigmoid_gate, silu_gate))


def gate_backward(grad_hidden, saved, scale_gate, scale_up):
    pre_gate, pre_up, gate_act, up_act, sigmoid_gate, silu_gate = saved
    grad_gate = grad_hidden * up_act * sigmoid_gate * (1.0 + gate_act * (1.0 - sigmoid_gate))
    grad_up = grad_hidden * silu_gate
    gate_logits = (grad_gate * scale_gate).astype(jnp.bfloat16)
    up_logits = (grad_up * scale_up).astype(jnp.bfloat16)
    return (
        gate_logits,
        up_logits,
        jnp.sum(grad_gate * pre_gate, axis=0),
        jnp.sum(grad_up * pre_up, axis=0),
    )


def per_device(
    tokens,
    frozen_gate_weight,
    frozen_up_weight,
    frozen_down_weight,
    gate_left_factor,
    gate_right_factor,
    up_left_factor,
    up_right_factor,
    down_left_factor,
    down_right_factor,
    gate_column_magnitude,
    up_column_magnitude,
    down_column_magnitude,
    cotangent,
):
    combined_gate_weight, gate_squared_columns = combine_adapter_columns(
        frozen_gate_weight, gate_left_factor, gate_right_factor
    )
    combined_up_weight, up_squared_columns = combine_adapter_columns(
        frozen_up_weight, up_left_factor, up_right_factor
    )
    combined_down_weight, down_squared_columns = combine_adapter_columns(
        frozen_down_weight, down_left_factor, down_right_factor
    )
    gate_squared_columns, up_squared_columns = lax.psum(
        (gate_squared_columns, up_squared_columns), "mp"
    )
    down_squared_columns = lax.psum(down_squared_columns, "dp")
    gate_column_norm = jnp.sqrt(gate_squared_columns + epsilon)
    up_column_norm = jnp.sqrt(up_squared_columns + epsilon)
    down_column_norm = jnp.sqrt(down_squared_columns + epsilon)
    scale_gate = gate_column_magnitude / gate_column_norm
    scale_up = up_column_magnitude / up_column_norm
    scale_down = down_column_magnitude / down_column_norm
    collected_rows = lax.all_gather(tokens, "dp", axis=0, tiled=True)
    local_rows = collected_rows.shape[0] // lax.axis_size("mp")
    row_start = lax.axis_index("mp") * local_rows
    gate_projection_output, up_projection_output = (
        lax.psum(
            matrix_product(collected_rows, gate_left_factor).astype(jnp.bfloat16), "mp"
        ).astype(jnp.float32),
        lax.psum(matrix_product(collected_rows, up_left_factor).astype(jnp.bfloat16), "mp").astype(
            jnp.float32
        ),
    )
    gate_projection_output = gate_projection_output.astype(jnp.bfloat16)
    up_projection_output = up_projection_output.astype(jnp.bfloat16)
    row_block = collected_rows
    pre_pair = lax.psum_scatter(
        jnp.concatenate(
            [
                matrix_product(row_block, combined_gate_weight),
                matrix_product(row_block, combined_up_weight),
            ],
            axis=1,
        ).astype(jnp.bfloat16),
        "mp",
        scatter_dimension=0,
        tiled=True,
    ).astype(jnp.float32)
    hidden_local, saved = activate(pre_pair, scale_gate, scale_up)
    hidden_state_full = lax.all_gather(hidden_local, "mp", axis=0, tiled=True)
    row_block = hidden_state_full
    down_preactivation = lax.psum_scatter(
        matrix_product(row_block, combined_down_weight).astype(jnp.bfloat16),
        "dp",
        scatter_dimension=0,
        tiled=True,
    ).astype(jnp.float32)
    feedforward_output = (down_preactivation * scale_down).astype(jnp.bfloat16)
    output_cotangent = cotangent.astype(jnp.float32)
    down_logits = (output_cotangent * scale_down).astype(jnp.bfloat16)
    down_projection_output, mag_down_sum = (
        lax.psum(
            matrix_product(hidden_state_full, down_left_factor).astype(jnp.bfloat16), "dp"
        ).astype(jnp.float32),
        lax.psum(
            jnp.sum(output_cotangent * down_preactivation, axis=0).astype(jnp.bfloat16), "dp"
        ).astype(jnp.float32),
    )
    down_projection_output = down_projection_output.astype(jnp.bfloat16)
    down_magnitude_gradient = mag_down_sum / down_column_norm
    down_logits_full = lax.all_gather(down_logits, "dp", axis=0, tiled=True)
    down_backward_rows = lax.psum(
        matrix_product_right_transposed(down_logits_full, down_right_factor).astype(jnp.bfloat16),
        "mp",
    )
    down_right_factor_gradient = matrix_product_left_transposed(
        down_projection_output, down_logits_full
    )
    down_left_factor_gradient = matrix_product_left_transposed(
        hidden_state_full, down_backward_rows
    )
    row_block = down_logits_full
    grad_hidden = lax.psum_scatter(
        matrix_product_right_transposed(row_block, combined_down_weight).astype(jnp.bfloat16),
        "mp",
        scatter_dimension=0,
        tiled=True,
    ).astype(jnp.float32)
    gate_logits, up_logits, mag_gate_terms, mag_up_terms = gate_backward(
        grad_hidden, saved, scale_gate, scale_up
    )
    proj_gate_rows = lax.dynamic_slice_in_dim(gate_projection_output, row_start, local_rows, 0)
    proj_up_rows = lax.dynamic_slice_in_dim(up_projection_output, row_start, local_rows, 0)
    gate_backward_rows, up_backward_rows = lax.psum(
        (
            matrix_product_right_transposed(gate_logits, gate_right_factor),
            matrix_product_right_transposed(up_logits, up_right_factor),
        ),
        "dp",
    )
    gate_backward_rows, up_backward_rows = (
        lax.all_gather(gate_backward_rows.astype(jnp.bfloat16), "mp", axis=0, tiled=True),
        lax.all_gather(up_backward_rows.astype(jnp.bfloat16), "mp", axis=0, tiled=True),
    )
    (
        gate_magnitude_total,
        up_magnitude_total,
        gate_right_factor_gradient,
        up_right_factor_gradient,
    ) = (
        lax.psum(mag_gate_terms.astype(jnp.bfloat16), "mp").astype(jnp.float32),
        lax.psum(mag_up_terms.astype(jnp.bfloat16), "mp").astype(jnp.float32),
        lax.psum(
            matrix_product_left_transposed(proj_gate_rows, gate_logits).astype(jnp.bfloat16), "mp"
        ).astype(jnp.float32),
        lax.psum(
            matrix_product_left_transposed(proj_up_rows, up_logits).astype(jnp.bfloat16), "mp"
        ).astype(jnp.float32),
    )
    z_gate_full, z_up_full = (
        lax.all_gather(gate_logits, "mp", axis=0, tiled=True),
        lax.all_gather(up_logits, "mp", axis=0, tiled=True),
    )
    gate_magnitude_gradient = gate_magnitude_total / gate_column_norm
    up_magnitude_gradient = up_magnitude_total / up_column_norm
    gate_left_factor_gradient = matrix_product_left_transposed(collected_rows, gate_backward_rows)
    up_left_factor_gradient = matrix_product_left_transposed(collected_rows, up_backward_rows)
    token_input_gradient = lax.psum_scatter(
        (
            matrix_product_right_transposed(z_gate_full, combined_gate_weight)
            + matrix_product_right_transposed(z_up_full, combined_up_weight)
        ).astype(jnp.bfloat16),
        "dp",
        scatter_dimension=0,
        tiled=True,
    )
    return (
        feedforward_output,
        token_input_gradient,
        gate_magnitude_gradient,
        up_magnitude_gradient,
        down_magnitude_gradient,
        gate_right_factor_gradient,
        gate_left_factor_gradient,
        up_right_factor_gradient,
        up_left_factor_gradient,
        down_right_factor_gradient,
        down_left_factor_gradient,
    )


def solution(mesh):
    placed = (
        P("dp", "mp"),
        P("mp", "dp"),
        P("mp", "dp"),
        P("dp", "mp"),
        P("mp", None),
        P(None, "dp"),
        P("mp", None),
        P(None, "dp"),
        P("dp", None),
        P(None, "mp"),
        P("dp"),
        P("dp"),
        P("mp"),
        P("dp", "mp"),
    )
    return jax.shard_map(
        per_device,
        mesh=mesh,
        in_specs=placed,
        out_specs=(
            P("dp", "mp"),
            P("dp", "mp"),
            P("dp"),
            P("dp"),
            P("mp"),
            P(None, "dp"),
            P("mp", None),
            P(None, "dp"),
            P("mp", None),
            P(None, "mp"),
            P("dp", None),
        ),
        check_vma=False,
    )
```

profile of v0, /device:TPU:0, one launch (start us, length us, event | category | flops | bytes accessed | tf_op | source)
XLA Modules:
  0.0 689.3 jit_solution(208738933042338539)
XLA Ops:
  7.2 9.0 %all_gather.21 = bf16[256,1024]{1,0:T(8,128)(2,1)S(1)} all-gather(bf16[64,1024]{1,0:T(8,128)(2,1)} %param.14), channel_id=1, replica_groups=mesh['dp'=4,'mp'=8] {'dp'}, dimensions={0}, use_global_device_ids=true | all-gather | bytes 655360 | tf_op jit(solution)/shard_map/all_gather | solution.py:94
  16.2 15.0 %multiply_reduce_fusion.1 = (f32[7168]{0:T(1024)S(1)}, f32[1024,7168]{1,0:T(8,128)}) fusion(bf16[1024,7168]{1,0:T(8,128)(2,1)} %param.16, bf16[1024,16]{0,1:T(8,128)(2,1)} %param.20, bf16[16,7168]{1,0:T(8,128)(2,1)} %param.21), kind=kOutput, calls=%fused_computation.2 | convolution fusion | flops 264233984 | bytes 44331008 | tf_op jit(solution)/shard_map/dot_general | solution.py:10
  31.2 18.4 %fusion.4 = bf16[256,7168]{0,1:T(8,128)(2,1)} fusion(bf16[256,1024]{1,0:T(8,128)(2,1)S(1)} %all_gather.21, f32[1024,7168]{1,0:T(8,128)} %get-tuple-element.34, bf16[1024,7168]{1,0:T(8,128)(2,1)} %param.16), kind=kOutput, calls=%fused_computation.13 | convolution fusion | flops 3781951488 | bytes 48234496 | tf_op jit(solution)/shard_map/dot_general | solution.py:10
  49.6 14.7 %multiply_reduce_fusion.2 = (f32[7168]{0:T(1024)S(1)}, f32[1024,7168]{1,0:T(8,128)}) fusion(bf16[1024,7168]{1,0:T(8,128)(2,1)} %param.15, bf16[1024,16]{0,1:T(8,128)(2,1)S(1)} %copy-done.6, bf16[16,7168]{1,0:T(8,128)(2,1)S(1)} %copy-done), kind=kOutput, calls=%fused_computation.3 | convolution fusion | flops 264233984 | bytes 44331008 | tf_op jit(solution)/shard_map/dot_general | solution.py:10
  64.4 18.4 %fusion.3 = bf16[256,7168]{0,1:T(8,128)(2,1)} fusion(bf16[256,1024]{1,0:T(8,128)(2,1)S(1)} %all_gather.21, f32[1024,7168]{1,0:T(8,128)} %get-tuple-element.36, bf16[1024,7168]{1,0:T(8,128)(2,1)} %param.15), kind=kOutput, calls=%fused_computation.12 | convolution fusion | flops 3781951488 | bytes 48234496 | tf_op jit(solution)/shard_map/dot_general | solution.py:10
  82.7 8.8 %pad_maximum_fusion = bf16[256,14336]{0,1:T(8,128)(2,1)} fusion(bf16[256,7168]{0,1:T(8,128)(2,1)} %fusion.4, bf16[256,7168]{0,1:T(8,128)(2,1)} %fusion.3), kind=kLoop, calls=%fused_computation.16 | loop fusion | flops 14680064 | bytes 14680064 | tf_op jit(solution)/shard_map/concatenate | solution.py:109
  91.5 10.2 %copy.40 = bf16[256,14336]{1,0:T(8,128)(2,1)} copy(bf16[256,14336]{0,1:T(8,128)(2,1)} %pad_maximum_fusion) | data formatting | bytes 14680064
  101.9 15.4 %multiply_reduce_fusion = (f32[1024]{0:T(1024)S(1)}, f32[7168,1024]{1,0:T(8,128)}) fusion(bf16[7168,1024]{1,0:T(8,128)(2,1)} %param.17, bf16[7168,16]{0,1:T(8,128)(2,1)S(1)} %copy-done.3, bf16[16,1024]{1,0:T(8,128)(2,1)S(1)} %copy-done.8), kind=kOutput, calls=%fused_computation | convolution fusion | flops 264240128 | bytes 44306432 | tf_op jit(solution)/shard_map/dot_general | solution.py:10
  117.2 7.1 %psum.100 = f32[1024]{0:T(1024)S(1)} all-reduce(f32[1024]{0:T(1024)S(1)} %get-tuple-element.31), channel_id=1, replica_groups=mesh['dp'=4,'mp'=8] {'dp'}, use_global_device_ids=true, to_apply=%region_7.0 | all-reduce | flops 1024 | bytes 8192 | tf_op jit(solution)/shard_map/psum | solution.py:87
  124.4 6.6 all_gather.23
  131.0 18.8 %convolution_convert_fusion.2 = bf16[256,7168]{1,0:T(8,128)(2,1)} fusion(bf16[256,1024]{1,0:T(8,128)(2,1)S(1)} %all_gather.23, f32[7168,1024]{1,0:T(8,128)} %get-tuple-element.32, bf16[7168,1024]{1,0:T(8,128)(2,1)} %param.17), kind=kOutput, calls=%fused_computation.11 | convolution fusion | flops 3781951488 | bytes 48234496 | tf_op jit(solution)/shard_map/dot_general | solution.py:14
  149.9 39.8 %all-reduce = (f32[7168]{0:T(1024)S(1)}, f32[7168]{0:T(1024)S(1)}) all-reduce(f32[7168]{0:T(1024)S(1)} %get-tuple-element.33, f32[7168]{0:T(1024)S(1)} %get-tuple-element.35), channel_id=1, replica_groups=mesh['dp'=4,'mp'=8] {'mp'}, use_global_device_ids=true, to_apply=%region_4.0 | all-reduce | flops 14336 | bytes 114688 | tf_op jit(solution)/shard_map/psum | solution.py:84
  190.6 47.0 %reduce-scatter.13.cloned.1.call-done = bf16[32,14336]{1,0:T(8,128)(2,1)} async-done(((bf16[256,14336]{1,0:T(8,128)(2,1)}), bf16[32,14336]{1,0:T(8,128)(2,1)}) %reduce-scatter.13.cloned.1.call-update) | async-done | bytes 917520 | tf_op jit(solution)/shard_map/reduce_scatter | solution.py:108
  237.5 2.6 convert_element_type.113
  240.1 81.1 %reduce-scatter.15.cloned.1.call-done = bf16[32,7168]{1,0:T(8,128)(2,1)} async-done(((bf16[256,7168]{1,0:T(8,128)(2,1)}), bf16[32,7168]{1,0:T(8,128)(2,1)}) %reduce-scatter.15.cloned.1.call-update) | async-done | bytes 458768 | tf_op jit(solution)/shard_map/reduce_scatter | solution.py:154
  321.2 3.0 multiply_reduce_fusion.3
  324.4 36.5 %all-reduce.2 = (bf16[7168]{0:T(1024)(128)(2,1)S(1)}, bf16[7168]{0:T(1024)(128)(2,1)S(1)}, bf16[256,16]{0,1:T(8,128)(2,1)S(1)}, bf16[256,16]{0,1:T(8,128)(2,1)S(1)}, bf16[256,16]{0,1:T(8,128)(2,1)S(1)}) all-reduce(bf16[7168]{0:T(1024)(128)(2,1)S(1)} %get-tuple-element.12, ...), channel_id=1, replica_groups=mesh['dp'=4,'mp'=8] {'mp'}, use_global_device_ids=true, to_apply=%region_11.0 | all-reduce | flops 26624 | bytes 106496 | tf_op jit(solution)/shard_map/psum | solution.py:182
  367.2 10.2 %all-reduce.1 = (bf16[32,16]{0,1:T(8,128)(2,1)S(1)}, bf16[32,16]{0,1:T(8,128)(2,1)S(1)}) all-reduce(f32[32,16]{0,1:T(8,128)S(1)} %fusion.27, f32[32,16]{0,1:T(8,128)S(1)} %fusion.28), channel_id=1, replica_groups=mesh['dp'=4,'mp'=8] {'dp'}, use_global_device_ids=true, to_apply=%region_18.0 | all-reduce | flops 1024 | bytes 6144 | tf_op jit(solution)/shard_map/psum | solution.py:165
  377.3 30.6 %all-gather = bf16[8,32,16]{1,2,0:T(8,128)(2,1)S(1)} all-gather(bf16[1,32,16]{1,2,0:T(8,128)(2,1)S(1)} %bitcast.55), channel_id=1, replica_groups=mesh['dp'=4,'mp'=8] {'mp'}, dimensions={0}, use_global_device_ids=true | all-gather | bytes 9216 | tf_op jit(solution)/shard_map/all_gather | solution.py:173
  408.0 30.6 %all-gather.1 = bf16[8,32,16]{1,2,0:T(8,128)(2,1)S(1)} all-gather(bf16[1,32,16]{1,2,0:T(8,128)(2,1)S(1)} %bitcast.54), channel_id=1, replica_groups=mesh['dp'=4,'mp'=8] {'mp'}, dimensions={0}, use_global_device_ids=true | all-gather | bytes 9216 | tf_op jit(solution)/shard_map/all_gather | solution.py:174
  441.0 1.8 convert_element_type.135
  442.8 1.7 convert_element_type.139
  444.5 56.3 %all-gather.6.cloned.1.call-done = bf16[256,7168]{1,0:T(8,128)(2,1)} async-done(((bf16[32,7168]{1,0:T(8,128)(2,1)}), bf16[256,7168]{1,0:T(8,128)(2,1)}) %all-gather.6.cloned.1.call-update) | async-done | bytes 3670032 | tf_op jit(solution)/shard_map/all_gather | solution.py:121
  500.9 18.0 %convolution_convert_fusion.5 = bf16[256,1024]{1,0:T(8,128)(2,1)} fusion(bf16[256,7168]{1,0:T(8,128)(2,1)} %all-gather.6.cloned.1.call-done, f32[7168,1024]{1,0:T(8,128)} %get-tuple-element.32, bf16[7168,1024]{1,0:T(8,128)(2,1)} %param.17), kind=kOutput, calls=%fused_computation.19 | convolution fusion | flops 3780378624 | bytes 48234496 | tf_op jit(solution)/shard_map/dot_general | solution.py:10
  518.9 48.9 %all-gather.8.cloned.1.call-done = bf16[256,7168]{1,0:T(8,128)(2,1)} async-done(((bf16[32,7168]{1,0:T(8,128)(2,1)}), bf16[256,7168]{1,0:T(8,128)(2,1)}) %all-gather.8.cloned.1.call-update) | async-done | bytes 3670032 | tf_op jit(solution)/shard_map/all_gather | solution.py:192
  567.9 16.5 %fusion.23 = f32[256,1024]{1,0:T(8,128)S(1)} fusion(bf16[256,7168]{1,0:T(8,128)(2,1)} %all-gather.8.cloned.1.call-done, f32[1024,7168]{1,0:T(8,128)} %get-tuple-element.36, bf16[1024,7168]{1,0:T(8,128)(2,1)} %param.15), kind=kOutput, calls=%fused_computation.60 | convolution fusion | flops 3780116480 | bytes 48758784 | tf_op jit(solution)/shard_map/dot_general | solution.py:14
  584.4 50.5 %all-gather.10.cloned.1.call-done = bf16[256,7168]{1,0:T(8,128)(2,1)} async-done(((bf16[32,7168]{1,0:T(8,128)(2,1)}), bf16[256,7168]{1,0:T(8,128)(2,1)}) %all-gather.10.cloned.1.call-update) | async-done | bytes 3670032 | tf_op jit(solution)/shard_map/all_gather | solution.py:193
  634.9 17.6 %fusion.5 = bf16[256,1024]{1,0:T(8,128)(2,1)} fusion(f32[256,1024]{1,0:T(8,128)S(1)} %fusion.23, bf16[256,7168]{1,0:T(8,128)(2,1)} %all-gather.10.cloned.1.call-done, f32[1024,7168]{1,0:T(8,128)} %get-tuple-element.34, bf16[1024,7168]{1,0:T(8,128)(2,1)} %param.16), kind=kOutput, calls=%fused_computation.18 | convolution fusion | flops 3780640768 | bytes 49283072 | tf_op jit(solution)/shard_map/dot_general | solution.py:14
  652.5 3.1 convolution_convert_fusion.6
  655.6 3.5 fusion.30
  660.6 10.1 %all-reduce.4 = (bf16[1024]{0:T(1024)(128)(2,1)S(1)}, bf16[256,16]{0,1:T(8,128)(2,1)S(1)}) all-reduce(bf16[1024]{0:T(1024)(128)(2,1)S(1)} %get-tuple-element.29, bf16[256,16]{0,1:T(8,128)(2,1)S(1)} %convolution_convert_fusion.6), channel_id=1, replica_groups=mesh['dp'=4,'mp'=8] {'dp'}, use_global_device_ids=true, to_apply=%region_15.0 | all-reduce | flops 5120 | bytes 20480 | tf_op jit(solution)/shard_map/psum | solution.py:136
  672.2 10.3 %reduce-scatter.11.cloned.1.call-done = bf16[64,1024]{1,0:T(8,128)(2,1)} async-done(((bf16[256,1024]{1,0:T(8,128)(2,1)}), bf16[64,1024]{1,0:T(8,128)(2,1)}) %reduce-scatter.11.cloned.1.call-update) | async-done | bytes 131088 | tf_op jit(solution)/shard_map/reduce_scatter | solution.py:199
  (64 shorter events, 12.9 us)
Async XLA Ops:
  7.2 42.5 %copy-start = (bf16[16,7168]{1,0:T(8,128)(2,1)S(1)}, bf16[16,7168]{1,0:T(8,128)(2,1)}, u32[]{:S(2)}) copy-start(bf16[16,7168]{1,0:T(8,128)(2,1)} %param.19) | copy-start | bytes 688132
  7.2 230.3 %reduce-scatter.13.cloned.1.call-start = ((), (), s32[]{:S(2)}) async-start(), calls=%async_computation.9 | async-start | bytes 8257536 | tf_op jit(solution)/shard_map/reduce_scatter | solution.py:108
  31.2 18.4 %copy-start.6 = (bf16[1024,16]{0,1:T(8,128)(2,1)S(1)}, bf16[1024,16]{0,1:T(8,128)(2,1)}, u32[]{:S(2)}) copy-start(bf16[1024,16]{0,1:T(8,128)(2,1)} %param.18) | copy-start | bytes 98308
  91.5 10.3 %copy-start.3 = (bf16[7168,16]{0,1:T(8,128)(2,1)S(1)}, bf16[7168,16]{0,1:T(8,128)(2,1)}, u32[]{:S(2)}) copy-start(bf16[7168,16]{0,1:T(8,128)(2,1)} %param.22) | copy-start | bytes 688132
  91.5 10.3 %copy-start.8 = (bf16[16,1024]{1,0:T(8,128)(2,1)S(1)}, bf16[16,1024]{1,0:T(8,128)(2,1)}, u32[]{:S(2)}) copy-start(bf16[16,1024]{1,0:T(8,128)(2,1)} %param.23) | copy-start | bytes 98308
  101.8 22.6 %copy-start.11 = (f32[1024]{0:T(1024)S(1)}, f32[1024]{0:T(1024)}, u32[]{:S(2)}) copy-start(f32[1024]{0:T(1024)} %param.26) | copy-start | bytes 12292
  101.8 22.6 %copy-start.5 = (bf16[64,1024]{1,0:T(8,128)(2,1)S(1)}, bf16[64,1024]{1,0:T(8,128)(2,1)}, u32[]{:S(2)}) copy-start(bf16[64,1024]{1,0:T(8,128)(2,1)} %param.27) | copy-start | bytes 393220
  101.8 219.4 %reduce-scatter.15.cloned.1.call-start = ((), (), s32[]{:S(2)}) async-start(), calls=%async_computation.10 | async-start | bytes 4128768 | tf_op jit(solution)/shard_map/reduce_scatter | solution.py:154
  131.0 58.7 %copy-start.9 = (f32[7168]{0:T(1024)S(1)}, f32[7168]{0:T(1024)}, u32[]{:S(2)}) copy-start(f32[7168]{0:T(1024)} %param.24) | copy-start | bytes 86020
  131.0 58.8 %copy-start.10 = (f32[7168]{0:T(1024)S(1)}, f32[7168]{0:T(1024)}, u32[]{:S(2)}) copy-start(f32[7168]{0:T(1024)} %param.25) | copy-start | bytes 86020
  131.0 59.0 %copy-start.7 = (bf16[1024,16]{0,1:T(8,128)(2,1)S(1)}, bf16[1024,16]{0,1:T(8,128)(2,1)}, u32[]{:S(2)}) copy-start(bf16[1024,16]{0,1:T(8,128)(2,1)} %param.20) | copy-start | bytes 98308
  149.9 216.0 %copy-start.4 = (bf16[16,7168]{1,0:T(8,128)(2,1)S(1)}, bf16[16,7168]{1,0:T(8,128)(2,1)}, u32[]{:S(2)}) copy-start(bf16[16,7168]{1,0:T(8,128)(2,1)} %param.21) | copy-start | bytes 688132
  149.9 291.1 %all-reduce.7.cloned.1.call-start = ((), (), s32[]{:S(2)}) async-start(), calls=%async_computation.11 | async-start | bytes 917504 | tf_op jit(solution)/shard_map/psum | solution.py:184
  324.3 39.8 %copy-start.1 = (bf16[32,7168]{1,0:T(8,128)(2,1)}, bf16[32,7168]{1,0:T(8,128)(2,1)S(1)}, u32[]{:S(2)}) copy-start(bf16[32,7168]{1,0:T(8,128)(2,1)S(1)} %get-tuple-element.27) | copy-start | bytes 1376260
  324.3 39.1 %copy-start.2 = (bf16[32,7168]{1,0:T(8,128)(2,1)}, bf16[32,7168]{1,0:T(8,128)(2,1)S(1)}, u32[]{:S(2)}) copy-start(bf16[32,7168]{1,0:T(8,128)(2,1)S(1)} %multiply_convert_fusion.1) | copy-start | bytes 1376260
  362.8 138.0 %all-gather.6.cloned.1.call-start = ((), (), s32[]{:S(2)}) async-start(), calls=%async_computation.4 | async-start | bytes 4128768 | tf_op jit(solution)/shard_map/all_gather | solution.py:121
  363.4 204.4 %all-gather.8.cloned.1.call-start = ((), (), s32[]{:S(2)}) async-start(), calls=%async_computation.6 | async-start | bytes 4128768 | tf_op jit(solution)/shard_map/all_gather | solution.py:192
  364.0 270.8 %all-gather.10.cloned.1.call-start = ((), (), s32[]{:S(2)}) async-start(), calls=%async_computation.7 | async-start | bytes 4128768 | tf_op jit(solution)/shard_map/all_gather | solution.py:193
  364.6 294.4 %reduce-scatter.9.cloned.1.call-start = ((), (), s32[]{:S(2)}) async-start(), calls=%async_computation.5 | async-start | bytes 655360 | tf_op jit(solution)/shard_map/reduce_scatter | solution.py:123
  518.9 163.6 %reduce-scatter.11.cloned.1.call-start = ((), (), s32[]{:S(2)}) async-start(), calls=%async_computation.8 | async-start | bytes 655360 | tf_op jit(solution)/shard_map/reduce_scatter | solution.py:199
Sparse Core Ops, SparseCore 0:
  101.9 135.5 reduce-scatter.12
  241.2 80.0 reduce-scatter.14
  363.0 69.7 all-reduce.6
  435.3 65.4 all-gather.5
  502.9 64.9 all-gather.7
  569.9 64.9 all-gather.9
  637.3 20.3 reduce-scatter.8
  660.8 21.6 reduce-scatter.10
where the time goes:
time: 690 us; the launch traced here: 689 us
  waiting for transfers between devices  296 us (43%)
  blocking collectives  181 us (26%)
  matrix products  167 us (24%)
  other arithmetic  20.9 us (3%)
  between operations  14.3 us (2%)
  local copies, waits for them, and re-layouts  10.5 us (2%)
    dot_general x9, matrix products, matrix_product(): return jnp.dot(left_side, right_side, preferred_element_type=jnp.float32)  103 us
    reduce_scatter x1, waiting for transfers between devices, per_device(): lax.psum_scatter(matrix_product_right_transposed(row_block, combined_down...  81.1 us
    all_gather x1, waiting for transfers between devices, per_device(): hidden_state_full = lax.all_gather(hidden_local, 'mp', axis=0, tiled=True)  56.3 us
    dot_general x6, matrix products, matrix_product_right_transposed(): lax.dot_general(left_side, right_side, (((1,), (1,)), ((), ())), preferre...  55.7 us
    all_gather x1, waiting for transfers between devices, per_device(): lax.all_gather(up_logits, 'mp', axis=0, tiled=True)  50.5 us
    all_gather x1, waiting for transfers between devices, per_device(): lax.all_gather(gate_logits, 'mp', axis=0, tiled=True)  48.9 us
    reduce_scatter x1, waiting for transfers between devices, per_device(): lax.psum_scatter(jnp.concatenate([matrix_product(row_block, combined_gate...  47 us
    psum x1, blocking collectives, per_device(): lax.psum((gate_squared_columns, up_squared_columns), 'mp')  39.8 us
  transfers between devices with their start and end apart: 8, of which 6 were waited for; matrix products, arithmetic and copies ran while one was open for 16% of the time, Pallas kernels for 0%

commit v1 on v0

--- a/solution.py
+++ b/solution.py
@@ -118,7 +118,12 @@
         tiled=True,
     ).astype(jnp.float32)
     hidden_local, saved = activate(pre_pair, scale_gate, scale_up)
-    hidden_state_full = lax.all_gather(hidden_local, "mp", axis=0, tiled=True)
+    ring = [hidden_local]
+    for hop in range(7):
+        ring.append(lax.ppermute(ring[-1], "mp", [(dev, (dev + 1) % 8) for dev in range(8)]))
+    hidden_state_full = jnp.roll(
+        jnp.concatenate(ring[::-1], axis=0), (lax.axis_index("mp") + 1) * ring[0].shape[0], axis=0
+    )
     row_block = hidden_state_full
     down_preactivation = lax.psum_scatter(
         matrix_product(row_block, combined_down_weight).astype(jnp.bfloat16),

time: 690 us -> 651 us (0.943)
  waiting for transfers between devices: 296 us -> 227 us
  local copies, waits for them, and re-layouts: 10.5 us -> 33.8 us
    ppermute x0 -> x7, waiting for transfers between devices: none -> 99.2 us  [per_device(): lax.ppermute(ring[-1], 'mp', [(dev, (dev + 1) % 8) for dev in range(8)])]
    all_gather x1 -> x0, waiting for transfers between devices: 56.3 us -> none  [per_device(): hidden_state_full = lax.all_gather(hidden_local, 'mp', axis=0, tiled=True)]
    all_gather x1, waiting for transfers between devices: 50.5 us -> 0.02 us  [per_device(): lax.all_gather(up_logits, 'mp', axis=0, tiled=True)]
    all_gather x1, waiting for transfers between devices: 48.9 us -> 0.02 us  [per_device(): lax.all_gather(gate_logits, 'mp', axis=0, tiled=True)]
    unnamed x27 -> x48, local copies, waits for them, and re-layouts: 10.5 us -> 33 us
    reduce_scatter x1, waiting for transfers between devices: 10.3 us -> 0.01 us  [per_device(): lax.psum_scatter((matrix_product_right_transposed(z_gate_full, combined_g...]
  transfers between devices with their start and end apart: 8 -> 14, of which waited for: 6 -> 8; matrix products, arithmetic and copies ran while one was open for 16% -> 20% of each run, Pallas kernels for 0% -> 0%
where the time goes in v1:
time: 651 us; the launch traced here: 649 us
  waiting for transfers between devices  227 us (35%)
  blocking collectives  183 us (28%)
  matrix products  167 us (26%)
  local copies, waits for them, and re-layouts  33.8 us (5%)
  other arithmetic  20.9 us (3%)
  between operations  14.4 us (2%)
    dot_general x9, matrix products, matrix_product(): return jnp.dot(left_side, right_side, preferred_element_type=jnp.float32)  103 us
    ppermute x7, waiting for transfers between devices, per_device(): lax.ppermute(ring[-1], 'mp', [(dev, (dev + 1) % 8) for dev in range(8)])  99.2 us
    reduce_scatter x1, waiting for transfers between devices, per_device(): lax.psum_scatter(matrix_product_right_transposed(row_block, combined_down...  81.1 us
    dot_general x6, matrix products, matrix_product_right_transposed(): lax.dot_general(left_side, right_side, (((1,), (1,)), ((), ())), preferre...  55.9 us
    reduce_scatter x1, waiting for transfers between devices, per_device(): lax.psum_scatter(jnp.concatenate([matrix_product(row_block, combined_gate...  46 us
    psum x1, blocking collectives, per_device(): lax.psum((gate_squared_columns, up_squared_columns), 'mp')  39.6 us
    psum x1, blocking collectives, per_device(): lax.psum(mag_gate_terms.astype(jnp.bfloat16), 'mp').astype(jnp.float32)  37.1 us
    unnamed x48, local copies, waits for them, and re-layouts  33 us
  transfers between devices with their start and end apart: 14, of which 8 were waited for; matrix products, arithmetic and copies ran while one was open for 20% of the time, Pallas kernels for 0%

profile of v1, /device:TPU:0, one launch (start us, length us, event | category | flops | bytes accessed | tf_op | source)
XLA Modules:
  0.0 649.2 jit_solution(14043339266614275368)
XLA Ops:
  7.2 9.0 %all_gather.18 = bf16[256,1024]{1,0:T(8,128)(2,1)S(1)} all-gather(bf16[64,1024]{1,0:T(8,128)(2,1)} %param.14), channel_id=1, replica_groups=mesh['dp'=4,'mp'=8] {'dp'}, dimensions={0}, use_global_device_ids=true | all-gather | bytes 655360 | tf_op jit(solution)/shard_map/all_gather | solution.py:94
  16.2 14.9 %multiply_reduce_fusion.2 = (f32[7168]{0:T(1024)S(1)}, f32[1024,7168]{1,0:T(8,128)}) fusion(bf16[1024,7168]{1,0:T(8,128)(2,1)} %param.15, bf16[1024,16]{0,1:T(8,128)(2,1)} %param.18, bf16[16,7168]{1,0:T(8,128)(2,1)} %param.19), kind=kOutput, calls=%fused_computation.3 | convolution fusion | flops 264233984 | bytes 44331008 | tf_op jit(solution)/shard_map/dot_general | solution.py:10
  31.2 18.4 %fusion.3 = bf16[256,7168]{0,1:T(8,128)(2,1)} fusion(bf16[256,1024]{1,0:T(8,128)(2,1)S(1)} %all_gather.18, f32[1024,7168]{1,0:T(8,128)} %get-tuple-element.36, bf16[1024,7168]{1,0:T(8,128)(2,1)} %param.15), kind=kOutput, calls=%fused_computation.12 | convolution fusion | flops 3781951488 | bytes 48234496 | tf_op jit(solution)/shard_map/dot_general | solution.py:10
  49.6 14.8 %multiply_reduce_fusion.1 = (f32[7168]{0:T(1024)S(1)}, f32[1024,7168]{1,0:T(8,128)}) fusion(bf16[1024,7168]{1,0:T(8,128)(2,1)} %param.16, bf16[1024,16]{0,1:T(8,128)(2,1)S(1)} %copy-done.7, bf16[16,7168]{1,0:T(8,128)(2,1)S(1)} %copy-done), kind=kOutput, calls=%fused_computation.2 | convolution fusion | flops 264233984 | bytes 44331008 | tf_op jit(solution)/shard_map/dot_general | solution.py:10
  64.4 18.4 %fusion.4 = bf16[256,7168]{0,1:T(8,128)(2,1)} fusion(bf16[256,1024]{1,0:T(8,128)(2,1)S(1)} %all_gather.18, f32[1024,7168]{1,0:T(8,128)} %get-tuple-element.34, bf16[1024,7168]{1,0:T(8,128)(2,1)} %param.16), kind=kOutput, calls=%fused_computation.13 | convolution fusion | flops 3781951488 | bytes 48234496 | tf_op jit(solution)/shard_map/dot_general | solution.py:10
  82.8 8.8 %pad_maximum_fusion = bf16[256,14336]{0,1:T(8,128)(2,1)} fusion(bf16[256,7168]{0,1:T(8,128)(2,1)} %fusion.4, bf16[256,7168]{0,1:T(8,128)(2,1)} %fusion.3), kind=kLoop, calls=%fused_computation.16 | loop fusion | flops 14680064 | bytes 14680064 | tf_op jit(solution)/shard_map/concatenate | solution.py:109
  91.6 10.0 %copy.54 = bf16[256,14336]{1,0:T(8,128)(2,1)} copy(bf16[256,14336]{0,1:T(8,128)(2,1)} %pad_maximum_fusion) | data formatting | bytes 14680064
  102.6 15.2 %multiply_reduce_fusion = (f32[1024]{0:T(1024)S(1)}, f32[7168,1024]{1,0:T(8,128)}) fusion(bf16[7168,1024]{1,0:T(8,128)(2,1)} %param.17, bf16[7168,16]{0,1:T(8,128)(2,1)S(1)} %copy-done.5, bf16[16,1024]{1,0:T(8,128)(2,1)S(1)} %copy-done.9), kind=kOutput, calls=%fused_computation | convolution fusion | flops 264240128 | bytes 44306432 | tf_op jit(solution)/shard_map/dot_general | solution.py:10
  117.7 7.1 %psum.100 = f32[1024]{0:T(1024)S(1)} all-reduce(f32[1024]{0:T(1024)S(1)} %get-tuple-element.31), channel_id=1, replica_groups=mesh['dp'=4,'mp'=8] {'dp'}, use_global_device_ids=true, to_apply=%region_7.0 | all-reduce | flops 1024 | bytes 8192 | tf_op jit(solution)/shard_map/psum | solution.py:87
  124.9 6.6 %all_gather.19 = bf16[256,1024]{1,0:T(8,128)(2,1)S(1)} all-gather(bf16[64,1024]{1,0:T(8,128)(2,1)S(1)} %fusion.22), channel_id=1, replica_groups=mesh['dp'=4,'mp'=8] {'dp'}, dimensions={0}, use_global_device_ids=true | all-gather | bytes 655360 | tf_op jit(solution)/shard_map/all_gather | solution.py:147
  131.5 18.7 %convolution_convert_fusion.2 = bf16[256,7168]{1,0:T(8,128)(2,1)} fusion(bf16[256,1024]{1,0:T(8,128)(2,1)S(1)} %all_gather.19, f32[7168,1024]{1,0:T(8,128)} %get-tuple-element.32, bf16[7168,1024]{1,0:T(8,128)(2,1)} %param.17), kind=kOutput, calls=%fused_computation.11 | convolution fusion | flops 3781951488 | bytes 48234496 | tf_op jit(solution)/shard_map/dot_general | solution.py:14
  150.3 39.6 %all-reduce = (f32[7168]{0:T(1024)S(1)}, f32[7168]{0:T(1024)S(1)}) all-reduce(f32[7168]{0:T(1024)S(1)} %get-tuple-element.33, f32[7168]{0:T(1024)S(1)} %get-tuple-element.35), channel_id=1, replica_groups=mesh['dp'=4,'mp'=8] {'mp'}, use_global_device_ids=true, to_apply=%region_4.0 | all-reduce | flops 14336 | bytes 114688 | tf_op jit(solution)/shard_map/psum | solution.py:84
  190.7 46.0 %reduce-scatter.13.cloned.1.call-done = bf16[32,14336]{1,0:T(8,128)(2,1)} async-done(((bf16[256,14336]{1,0:T(8,128)(2,1)}), bf16[32,14336]{1,0:T(8,128)(2,1)}) %reduce-scatter.13.cloned.1.call-update) | async-done | bytes 917520 | tf_op jit(solution)/shard_map/reduce_scatter | solution.py:108
  236.7 2.5 convert_element_type.113
  239.2 81.1 %reduce-scatter.15.cloned.1.call-done = bf16[32,7168]{1,0:T(8,128)(2,1)} async-done(((bf16[256,7168]{1,0:T(8,128)(2,1)}), bf16[32,7168]{1,0:T(8,128)(2,1)}) %reduce-scatter.15.cloned.1.call-update) | async-done | bytes 458768 | tf_op jit(solution)/shard_map/reduce_scatter | solution.py:159
  320.3 2.4 multiply_reduce_fusion.3
  322.8 37.1 %all-reduce.2 = (bf16[7168]{0:T(1024)(128)(2,1)}, bf16[7168]{0:T(1024)(128)(2,1)}, bf16[256,16]{0,1:T(8,128)(2,1)S(1)}, bf16[256,16]{0,1:T(8,128)(2,1)S(1)}, bf16[256,16]{0,1:T(8,128)(2,1)}) all-reduce(bf16[7168]{0:T(1024)(128)(2,1)S(1)} %get-tuple-element.12, ...), channel_id=1, replica_groups=mesh['dp'=4,'mp'=8] {'mp'}, use_global_device_ids=true, to_apply=%region_11.12 | all-reduce | flops 26624 | bytes 106496 | tf_op jit(solution)/shard_map/psum | solution.py:187
  362.5 19.9 %collective-permute-done = bf16[32,7168]{1,0:T(8,128)(2,1)S(1)} collective-permute-done((bf16[32,7168]{1,0:T(8,128)(2,1)S(1)}, bf16[32,7168]{1,0:T(8,128)(2,1)S(1)}, u32[]{:S(2)}, u32[]{:S(2)}) %collective-permute-start) | collective-permute-done | bytes 458784 | tf_op jit(solution)/shard_map/ppermute | solution.py:123
  382.5 17.2 %collective-permute-done.1 = bf16[32,7168]{1,0:T(8,128)(2,1)S(1)} collective-permute-done((bf16[32,7168]{1,0:T(8,128)(2,1)S(1)}, bf16[32,7168]{1,0:T(8,128)(2,1)S(1)}, u32[]{:S(2)}, u32[]{:S(2)}) %collective-permute-start.1) | collective-permute-done | bytes 458784 | tf_op jit(solution)/shard_map/ppermute | solution.py:123
  399.7 16.4 %collective-permute-done.2 = bf16[32,7168]{1,0:T(8,128)(2,1)S(1)} collective-permute-done((bf16[32,7168]{1,0:T(8,128)(2,1)S(1)}, bf16[32,7168]{1,0:T(8,128)(2,1)S(1)}, u32[]{:S(2)}, u32[]{:S(2)}) %collective-permute-start.2) | collective-permute-done | bytes 458784 | tf_op jit(solution)/shard_map/ppermute | solution.py:123
  416.9 14.8 %collective-permute-done.3 = bf16[32,7168]{1,0:T(8,128)(2,1)} collective-permute-done((bf16[32,7168]{1,0:T(8,128)(2,1)S(1)}, bf16[32,7168]{1,0:T(8,128)(2,1)}, u32[]{:S(2)}, u32[]{:S(2)}) %collective-permute-start.3) | collective-permute-done | bytes 458784 | tf_op jit(solution)/shard_map/ppermute | solution.py:123
  433.1 17.2 %collective-permute-done.4 = bf16[32,7168]{1,0:T(8,128)(2,1)} collective-permute-done((bf16[32,7168]{1,0:T(8,128)(2,1)}, bf16[32,7168]{1,0:T(8,128)(2,1)}, u32[]{:S(2)}, u32[]{:S(2)}) %collective-permute-start.4) | collective-permute-done | bytes 458784 | tf_op jit(solution)/shard_map/ppermute | solution.py:123
  452.2 10.6 %all-reduce.1 = (bf16[32,16]{0,1:T(8,128)(2,1)S(1)}, bf16[32,16]{0,1:T(8,128)(2,1)S(1)}) all-reduce(f32[32,16]{0,1:T(8,128)} %fusion.42, f32[32,16]{0,1:T(8,128)S(1)} %fusion.43), channel_id=1, replica_groups=mesh['dp'=4,'mp'=8] {'dp'}, use_global_device_ids=true, to_apply=%region_18.19 | all-reduce | flops 1024 | bytes 6144 | tf_op jit(solution)/shard_map/psum | solution.py:170
  462.8 31.3 %all-gather.1 = bf16[8,32,16]{1,2,0:T(8,128)(2,1)S(1)} all-gather(bf16[1,32,16]{1,2,0:T(8,128)(2,1)S(1)} %bitcast.52), channel_id=1, replica_groups=mesh['dp'=4,'mp'=8] {'mp'}, dimensions={0}, use_global_device_ids=true | all-gather | bytes 9216 | tf_op jit(solution)/shard_map/all_gather | solution.py:179
  494.2 31.4 %all-gather = bf16[8,32,16]{1,2,0:T(8,128)(2,1)S(1)} all-gather(bf16[1,32,16]{1,2,0:T(8,128)(2,1)S(1)} %bitcast.51), channel_id=1, replica_groups=mesh['dp'=4,'mp'=8] {'mp'}, dimensions={0}, use_global_device_ids=true | all-gather | bytes 9216 | tf_op jit(solution)/shard_map/all_gather | solution.py:178
  535.5 13.6 %collective-permute-done.6 = bf16[32,7168]{1,0:T(8,128)(2,1)} collective-permute-done((bf16[32,7168]{1,0:T(8,128)(2,1)}, bf16[32,7168]{1,0:T(8,128)(2,1)}, u32[]{:S(2)}, u32[]{:S(2)}) %collective-permute-start.6) | collective-permute-done | bytes 458784 | tf_op jit(solution)/shard_map/ppermute | solution.py:123
  570.4 17.7 %fusion.12 = bf16[256,1024]{1,0:T(8,128)(2,1)} fusion(bf16[512,7168]{1,0:T(8,128)(2,1)} %constant_dynamic-update-slice_fusion, s32[]{:T(128)S(6)} %select_n.18, f32[7168,1024]{1,0:T(8,128)} %get-tuple-element.32, bf16[7168,1024]{1,0:T(8,128)(2,1)} %param.17), kind=kOutput, calls=%fused_computation.25 | convolution fusion | flops 3780378624 | bytes 48234500 | tf_op jit(solution)/shard_map/dot_general | solution.py:10
  588.2 16.3 %fusion.38 = f32[256,1024]{1,0:T(8,128)S(1)} fusion(bf16[256,7168]{1,0:T(8,128)(2,1)} %all-gather.5.cloned.1.call-done, f32[1024,7168]{1,0:T(8,128)} %get-tuple-element.36, bf16[1024,7168]{1,0:T(8,128)(2,1)} %param.15), kind=kOutput, calls=%fused_computation.85 | convolution fusion | flops 3780116480 | bytes 48758784 | tf_op jit(solution)/shard_map/dot_general | solution.py:14
  604.5 17.4 %fusion.11 = bf16[256,1024]{1,0:T(8,128)(2,1)} fusion(f32[256,1024]{1,0:T(8,128)S(1)} %fusion.38, bf16[256,7168]{1,0:T(8,128)(2,1)} %all-gather.7.cloned.1.call-done, f32[1024,7168]{1,0:T(8,128)} %get-tuple-element.34, bf16[1024,7168]{1,0:T(8,128)(2,1)} %param.16), kind=kOutput, calls=%fused_computation.24 | convolution fusion | flops 3780640768 | bytes 49283072 | tf_op jit(solution)/shard_map/dot_general | solution.py:14
  622.0 3.1 fusion.15
  625.1 3.5 fusion.5
  630.2 10.7 %all-reduce.4 = (bf16[1024]{0:T(1024)(128)(2,1)S(1)}, bf16[256,16]{0,1:T(8,128)(2,1)S(1)}) all-reduce(bf16[1024]{0:T(1024)(128)(2,1)S(1)} %get-tuple-element.29, bf16[256,16]{0,1:T(8,128)(2,1)S(1)} %fusion.15), channel_id=1, replica_groups=mesh['dp'=4,'mp'=8] {'dp'}, use_global_device_ids=true, to_apply=%region_15.16 | all-reduce | flops 5120 | bytes 20480 | tf_op jit(solution)/shard_map/psum | solution.py:141
  (97 shorter events, 42.9 us)
Async XLA Ops:
  7.2 42.4 %copy-start = (bf16[16,7168]{1,0:T(8,128)(2,1)S(1)}, bf16[16,7168]{1,0:T(8,128)(2,1)}, u32[]{:S(2)}) copy-start(bf16[16,7168]{1,0:T(8,128)(2,1)} %param.21) | copy-start | bytes 688132
  7.2 229.5 %reduce-scatter.13.cloned.1.call-start = ((), (), s32[]{:S(2)}) async-start(), calls=%async_computation.8 | async-start | bytes 8257536 | tf_op jit(solution)/shard_map/reduce_scatter | solution.py:108
  31.2 18.4 %copy-start.7 = (bf16[1024,16]{0,1:T(8,128)(2,1)S(1)}, bf16[1024,16]{0,1:T(8,128)(2,1)}, u32[]{:S(2)}) copy-start(bf16[1024,16]{0,1:T(8,128)(2,1)} %param.20) | copy-start | bytes 98308
  101.6 0.9 copy-start.5
  101.6 0.9 copy-start.9
  101.7 23.2 %copy-start.14 = (f32[1024]{0:T(1024)S(1)}, f32[1024]{0:T(1024)}, u32[]{:S(2)}) copy-start(f32[1024]{0:T(1024)} %param.26) | copy-start | bytes 12292
  101.7 23.2 %copy-start.6 = (bf16[64,1024]{1,0:T(8,128)(2,1)S(1)}, bf16[64,1024]{1,0:T(8,128)(2,1)}, u32[]{:S(2)}) copy-start(bf16[64,1024]{1,0:T(8,128)(2,1)} %param.27) | copy-start | bytes 393220
  101.7 218.7 %reduce-scatter.15.cloned.1.call-start = ((), (), s32[]{:S(2)}) async-start(), calls=%async_computation.9 | async-start | bytes 4128768 | tf_op jit(solution)/shard_map/reduce_scatter | solution.py:159
  131.5 58.4 %copy-start.11 = (f32[7168]{0:T(1024)S(1)}, f32[7168]{0:T(1024)}, u32[]{:S(2)}) copy-start(f32[7168]{0:T(1024)} %param.24) | copy-start | bytes 86020
  131.5 58.4 %copy-start.12 = (f32[7168]{0:T(1024)S(1)}, f32[7168]{0:T(1024)}, u32[]{:S(2)}) copy-start(f32[7168]{0:T(1024)} %param.25) | copy-start | bytes 86020
  131.5 58.7 %copy-start.8 = (bf16[1024,16]{0,1:T(8,128)(2,1)S(1)}, bf16[1024,16]{0,1:T(8,128)(2,1)}, u32[]{:S(2)}) copy-start(bf16[1024,16]{0,1:T(8,128)(2,1)} %param.18) | copy-start | bytes 98308
  150.3 381.7 %all-reduce.7.cloned.1.call-start = ((), (), s32[]{:S(2)}) async-start(), calls=%async_computation.10 | async-start | bytes 917504 | tf_op jit(solution)/shard_map/psum | solution.py:189
  189.9 272.9 %copy-start.10 = (f32[7168]{0:T(1024)}, f32[7168]{0:T(1024)S(1)}, u32[]{:S(2)}) copy-start(f32[7168]{0:T(1024)S(1)} %get-tuple-element.14) | copy-start | bytes 86020
  322.7 109.0 %copy-start.1 = (bf16[32,7168]{1,0:T(8,128)(2,1)}, bf16[32,7168]{1,0:T(8,128)(2,1)S(1)}, u32[]{:S(2)}) copy-start(bf16[32,7168]{1,0:T(8,128)(2,1)S(1)} %get-tuple-element.27) | copy-start | bytes 1376260
  322.8 39.1 %copy-start.2 = (bf16[32,7168]{1,0:T(8,128)(2,1)}, bf16[32,7168]{1,0:T(8,128)(2,1)S(1)}, u32[]{:S(2)}) copy-start(bf16[32,7168]{1,0:T(8,128)(2,1)S(1)} %multiply_convert_fusion.1) | copy-start | bytes 1376260
  361.9 226.3 %all-gather.5.cloned.1.call-start = ((), (), s32[]{:S(2)}) async-start(), calls=%async_computation.5 | async-start | bytes 4128768 | tf_op jit(solution)/shard_map/all_gather | solution.py:197
  362.4 242.1 %all-gather.7.cloned.1.call-start = ((), (), s32[]{:S(2)}) async-start(), calls=%async_computation.6 | async-start | bytes 4128768 | tf_op jit(solution)/shard_map/all_gather | solution.py:198
  362.5 20.0 %collective-permute-start = (bf16[32,7168]{1,0:T(8,128)(2,1)S(1)}, bf16[32,7168]{1,0:T(8,128)(2,1)S(1)}, u32[]{:S(2)}, u32[]{:S(2)}) collective-permute-start(bf16[32,7168]{1,0:T(8,128)(2,1)S(1)} %get-tuple-element.28), channel_id=1, source_target_pairs={{0,1},{1,2},{2,3},{3,4},{4,5},{5,6},{6,7},{7,0},{8,9},{9,10},{10,1... | collective-permute-start | bytes 1376264 | tf_op jit(solution)/shard_map/ppermute | solution.py:123
  382.5 17.2 %collective-permute-start.1 = (bf16[32,7168]{1,0:T(8,128)(2,1)S(1)}, bf16[32,7168]{1,0:T(8,128)(2,1)S(1)}, u32[]{:S(2)}, u32[]{:S(2)}) collective-permute-start(bf16[32,7168]{1,0:T(8,128)(2,1)S(1)} %collective-permute-done), channel_id=1, source_target_pairs={{0,1},{1,2},{2,3},{3,4},{4,5},{5,6},{6,7},{7,0},{8,9},{9,10},{10,1... | collective-permute-start | bytes 1376264 | tf_op jit(solution)/shard_map/ppermute | solution.py:123
  399.7 16.4 %collective-permute-start.2 = (bf16[32,7168]{1,0:T(8,128)(2,1)S(1)}, bf16[32,7168]{1,0:T(8,128)(2,1)S(1)}, u32[]{:S(2)}, u32[]{:S(2)}) collective-permute-start(bf16[32,7168]{1,0:T(8,128)(2,1)S(1)} %collective-permute-done.1), channel_id=1, source_target_pairs={{0,1},{1,2},{2,3},{3,4},{4,5},{5,6},{6,7},{7,0},{8,9},{9,10},{10,1... | collective-permute-start | bytes 1376264 | tf_op jit(solution)/shard_map/ppermute | solution.py:123
  416.1 0.8 copy-start.3
  416.9 14.8 %collective-permute-start.3 = (bf16[32,7168]{1,0:T(8,128)(2,1)S(1)}, bf16[32,7168]{1,0:T(8,128)(2,1)}, u32[]{:S(2)}, u32[]{:S(2)}) collective-permute-start(bf16[32,7168]{1,0:T(8,128)(2,1)S(1)} %collective-permute-done.2), channel_id=1, source_target_pairs={{0,1},{1,2},{2,3},{3,4},{4,5},{5,6},{6,7},{7,0},{8,9},{9,10},{10,1... | collective-permute-start | bytes 1376264 | tf_op jit(solution)/shard_map/ppermute | solution.py:123
  431.7 18.6 %collective-permute-start.4 = (bf16[32,7168]{1,0:T(8,128)(2,1)}, bf16[32,7168]{1,0:T(8,128)(2,1)}, u32[]{:S(2)}, u32[]{:S(2)}) collective-permute-start(bf16[32,7168]{1,0:T(8,128)(2,1)} %collective-permute-done.3), channel_id=1, source_target_pairs={{0,1},{1,2},{2,3},{3,4},{4,5},{5,6},{6,7},{7,0},{8,9},{9,10},{10,1... | collective-permute-start | bytes 1376264 | tf_op jit(solution)/shard_map/ppermute | solution.py:123
  431.7 124.9 %copy-start.4 = (bf16[32,7168]{1,0:T(8,128)(2,1)S(1)}, bf16[32,7168]{1,0:T(8,128)(2,1)}, u32[]{:S(2)}) copy-start(bf16[32,7168]{1,0:T(8,128)(2,1)} %copy-done.3) | copy-start | bytes 1376260
  431.8 196.8 %reduce-scatter.9.cloned.1.call-start = ((), (), s32[]{:S(2)}) async-start(), calls=%async_computation.4 | async-start | bytes 655360 | tf_op jit(solution)/shard_map/reduce_scatter | solution.py:128
  450.3 77.6 %collective-permute-start.5 = (bf16[32,7168]{1,0:T(8,128)(2,1)}, bf16[32,7168]{1,0:T(8,128)(2,1)}, u32[]{:S(2)}, u32[]{:S(2)}) collective-permute-start(bf16[32,7168]{1,0:T(8,128)(2,1)} %collective-permute-done.4), channel_id=1, source_target_pairs={{0,1},{1,2},{2,3},{3,4},{4,5},{5,6},{6,7},{7,0},{8,9},{9,10},{10,1... | collective-permute-start | bytes 1376264 | tf_op jit(solution)/shard_map/ppermute | solution.py:123
  527.9 21.2 %collective-permute-start.6 = (bf16[32,7168]{1,0:T(8,128)(2,1)}, bf16[32,7168]{1,0:T(8,128)(2,1)}, u32[]{:S(2)}, u32[]{:S(2)}) collective-permute-start(bf16[32,7168]{1,0:T(8,128)(2,1)} %collective-permute-done.5), channel_id=1, source_target_pairs={{0,1},{1,2},{2,3},{3,4},{4,5},{5,6},{6,7},{7,0},{8,9},{9,10},{10,1... | collective-permute-start | bytes 1376264 | tf_op jit(solution)/shard_map/ppermute | solution.py:123
  588.1 54.3 %reduce-scatter.11.cloned.1.call-start = ((), (), s32[]{:S(2)}) async-start(), calls=%async_computation.7 | async-start | bytes 655360 | tf_op jit(solution)/shard_map/reduce_scatter | solution.py:204
  604.5 20.6 %copy-start.13 = (bf16[256,16]{0,1:T(8,128)(2,1)S(1)}, bf16[256,16]{0,1:T(8,128)(2,1)}, u32[]{:S(2)}) copy-start(bf16[256,16]{0,1:T(8,128)(2,1)} %get-tuple-element.21) | copy-start | bytes 24580
Sparse Core Ops, SparseCore 0:
  101.8 134.8 reduce-scatter.12
  240.3 79.9 reduce-scatter.14
  362.0 81.2 all-reduce.6
  445.4 69.4 all-gather.4
  516.9 69.5 all-gather.6
  588.8 20.3 reduce-scatter.8
  622.1 19.0 reduce-scatter.10
